TPU v7x, 32 devices: a whole 2x2x4 slice. The times are simulated.
32 devices in a mesh: gx: 2 (over y), gy: 4 (over x, core), gz: 4 (over z).
Axes of the slice: x: 2, y: 2, z: 4, core: 2. Of those that a mesh axis runs over, the one named last changes fastest.
Arguments:
- head_out: bfloat16 [768, 4096], P(('gy', 'gx'), 'gz'), may hold values from -6 to 6
- out_weight: bfloat16 [4096, 4096], P('gz', ('gx', 'gy')), may hold values from -0.09375 to 0.09375
- residual: bfloat16 [768, 4096], P(('gy', 'gz'), 'gx'), may hold values from -84 to 84
- norm_gain: bfloat16 [4096], replicated, may hold values from 0.5 to 1.5
Outputs:
- hidden_out: bfloat16 [768, 4096], P(('gy', 'gz'), 'gx')
- normed: bfloat16 [768, 4096], P(('gy', 'gz'), 'gx')
All inputs are finite; a program needn't handle non-finite values.
Results may differ from a plain program's by a relative error of at most 0.0098.
Values may be sent and summed in bfloat16 or wider, within the bound.
A program may use at most 64 MiB of HBM per device.

v0:
```python
import functools

import jax
import jax.numpy as jnp
from jax import lax
from jax.experimental import pallas as pl
from jax.experimental.pallas import tpu as pltpu
from jax.sharding import PartitionSpec as P

MESH = pl.DeviceIdType.MESH
F32 = jnp.float32
BF16 = jnp.bfloat16
CORES = 2


def kernel(ny, ngy, nz, head_ref, w_ref, res_ref, gain_ref, hid_ref, nrm_ref,
           heads, w_own, w_other, res_v, send_buf, recv, own, sums,
           local_sem, w_send, w_recv, h_send, h_recv, p_send, p_recv, s_send, s_recv):
    nx = ngy // CORES
    y = lax.axis_index("gx")
    gy = lax.axis_index("gy")
    z = lax.axis_index("gz")
    x, core = lax.div(gy, CORES), lax.rem(gy, CORES)
    in_rows = head_ref.shape[0]
    out_rows, cols = res_ref.shape
    wc = w_ref.shape[1]
    per_block = nz // ny

    def at(dx, dy, dz):
        return (lax.rem(y + dy + ny, ny), lax.rem(x + dx + nx, nx) * CORES + core, lax.rem(z + dz + nz, nz))

    partner = (y, x * CORES + 1 - core, z)
    offsets = {(dx, dy, 0) for dx in range(nx) for dy in range(ny)} | {(dx, 0, dz) for dx in range(nx) for dz in range(nz)}
    offsets = sorted(offsets - {(0, 0, 0)})
    barrier = pltpu.get_barrier_semaphore()
    pl.semaphore_signal(barrier, inc=1, device_id=partner, device_id_type=MESH)
    for off in offsets:
        pl.semaphore_signal(barrier, inc=1, device_id=at(*off), device_id_type=MESH)

    head_in = pltpu.make_async_copy(head_ref, heads.at[0, 0], local_sem.at[0])
    w_in = pltpu.make_async_copy(w_ref, w_own, local_sem.at[1])
    res_in = pltpu.make_async_copy(res_ref, res_v, local_sem.at[2])
    head_in.start()
    w_in.start()
    res_in.start()
    head_in.wait()
    pl.semaphore_wait(barrier, len(offsets) + 1)

    blocks = sorted(((dx, dy) for dx in range(nx) for dy in range(ny)), key=lambda b: ((b[0] > 0) + (b[1] > 0), b))
    head_copies = {}
    for dx, dy in blocks[1:]:
        head_copies[dx, dy] = pltpu.make_async_remote_copy(
            src_ref=heads.at[0, 0], dst_ref=heads.at[dx, dy],
            send_sem=h_send.at[dx, dy], recv_sem=h_recv.at[dx, dy],
            device_id=at(-dx, -dy, 0), device_id_type=MESH)
        head_copies[dx, dy].start()
    w_in.wait()
    w_copy = pltpu.make_async_remote_copy(
        src_ref=w_own, dst_ref=w_other, send_sem=w_send, recv_sem=w_recv,
        device_id=partner, device_id_type=MESH)
    w_copy.start()

    def chunk(dx, dy, hr, j):
        to_z = lax.rem(y + dy, ny) * per_block + j
        dz = lax.rem(to_z - z + nz, nz)
        copy = pltpu.make_async_remote_copy(
            src_ref=send_buf.at[dx, dy, hr, pl.ds(j * out_rows, out_rows)],
            dst_ref=recv.at[dx, dz, hr],
            send_sem=p_send.at[dx, dy, hr, j], recv_sem=p_recv.at[dx, dz, hr],
            device_id=(y, lax.rem(x + dx, nx) * CORES + core, to_z), device_id_type=MESH)
        return to_z, copy

    for dx, dy in blocks:
        if (dx, dy) != (0, 0):
            head_copies[dx, dy].wait_recv()
        for hr in range(CORES):
            if (dx, dy) == (0, 0) and hr == 1:
                w_copy.wait_recv()
            part = jnp.dot(heads[dx, dy], (w_other if hr else w_own)[...], preferred_element_type=F32)
            send_buf[dx, dy, hr] = part.astype(BF16)
            for j in range(per_block):
                to_z, copy = chunk(dx, dy, hr, j)
                if dx:
                    copy.start()
                else:
                    pl.when(to_z != z)(copy.start)

                    @pl.when(to_z == z)
                    def _():
                        own[hr] = part[j * out_rows:(j + 1) * out_rows]

    res_in.wait()
    total = jnp.zeros((out_rows, 128), F32)
    for dx in range(nx):
        from_x = lax.rem(x - dx + nx, nx)
        for hr in range(CORES):
            half = core if hr == 0 else 1 - core
            where = pl.ds(pl.multiple_of((from_x * CORES + half) * wc, wc), wc)
            acc = own[hr] if dx == 0 else None
            for dz in range(nz):
                if (dx, dz) == (0, 0):
                    continue
                pltpu.make_async_remote_copy(
                    src_ref=send_buf.at[0, 0, hr, pl.ds(0, out_rows)], dst_ref=recv.at[dx, dz, hr],
                    send_sem=p_send.at[0, 0, hr, 0], recv_sem=p_recv.at[dx, dz, hr],
                    device_id=partner, device_id_type=MESH).wait_recv()
                term = recv[dx, dz, hr].astype(F32)
                acc = term if acc is None else acc + term
            hidden = (res_v[:, where].astype(F32) + acc).astype(BF16)
            hid_ref[:, where] = hidden
            wide = hidden.astype(F32)
            square = wide * wide
            for k in range(0, wc, 128):
                total = total + square[:, k:k + 128]
    sums[0] = jnp.broadcast_to(jnp.sum(total, axis=1, keepdims=True), (out_rows, 128))
    sum_copies = []
    for dy in range(1, ny):
        sum_copies.append(pltpu.make_async_remote_copy(
            src_ref=sums.at[0], dst_ref=sums.at[dy], send_sem=s_send.at[dy], recv_sem=s_recv.at[dy],
            device_id=at(0, -dy, 0), device_id_type=MESH))
        sum_copies[-1].start()

    w_copy.wait_send()
    for copy in head_copies.values():
        copy.wait_send()
    for dx, dy in blocks:
        for hr in range(CORES):
            for j in range(per_block):
                to_z, copy = chunk(dx, dy, hr, j)
                if dx:
                    copy.wait_send()
                else:
                    pl.when(to_z != z)(copy.wait_send)
    squares = sums[0]
    for dy, copy in enumerate(sum_copies, 1):
        copy.wait()
        squares = squares + sums[dy]
    inverse = lax.rsqrt(squares / (cols * ny) + 1e-05)[:, :1]
    gain = gain_ref[pl.ds(pl.multiple_of(y * cols, cols), cols)].astype(F32).reshape(1, cols)
    nrm_ref[...] = (hid_ref[...].astype(F32) * inverse * gain).astype(BF16)


def shards(head_out, out_weight, residual, norm_gain):
    ny, ngy, nz = (lax.axis_size(a) for a in ("gx", "gy", "gz"))
    nx = ngy // CORES
    in_rows, depth = head_out.shape
    wc = out_weight.shape[1]
    out_rows, cols = residual.shape
    per_block = nz // ny
    any_spec = pl.BlockSpec(memory_space=pl.ANY)
    vmem = pl.BlockSpec(memory_space=pltpu.VMEM)
    dma = pltpu.SemaphoreType.DMA
    return pl.pallas_call(
        functools.partial(kernel, ny, ngy, nz),
        out_shape=[jax.ShapeDtypeStruct((out_rows, cols), BF16)] * 2,
        in_specs=[any_spec, any_spec, any_spec, vmem],
        out_specs=[vmem, vmem],
        scratch_shapes=[
            pltpu.VMEM((nx, ny, in_rows, depth), BF16),
            pltpu.VMEM((depth, wc), BF16),
            pltpu.VMEM((depth, wc), BF16),
            pltpu.VMEM((out_rows, cols), BF16),
            pltpu.VMEM((nx, ny, CORES, in_rows, wc), BF16),
            pltpu.VMEM((nx, nz, CORES, out_rows, wc), BF16),
            pltpu.VMEM((CORES, out_rows, wc), F32),
            pltpu.VMEM((ny, out_rows, 128), F32),
            dma((3,)), dma, dma, dma((nx, ny)), dma((nx, ny)),
            dma((nx, ny, CORES, per_block)), dma((nx, nz, CORES)),
            dma((ny,)), dma((ny,)),
        ],
        compiler_params=pltpu.CompilerParams(collective_id=0, has_side_effects=True),
    )(head_out, out_weight, residual, norm_gain)


def solution(mesh):
    in_specs = (P(("gy", "gx"), "gz"), P("gz", ("gx", "gy")), P(("gy", "gz"), "gx"), P())
    out_specs = (P(("gy", "gz"), "gx"), P(("gy", "gz"), "gx"))
    return jax.shard_map(shards, mesh=mesh, in_specs=in_specs, out_specs=out_specs, check_vma=False)
```

profile of v0, /device:TPU:0, one launch (start us, length us, event | category | flops | bytes accessed | tf_op | source)
XLA Modules:
  0.0 36.6 jit_solution(13728688314581159124)
XLA Ops:
  0.6 33.6 %shard_map.59 = (bf16[48,2048]{1,0:T(8,128)(2,1)}, bf16[48,2048]{1,0:T(8,128)(2,1)}) custom-call(bf16[96,1024]{1,0:T(8,128)(2,1)} %head_ref.1, bf16[1024,512]{1,0:T(8,128)(2,1)} %w_ref.1, bf16[48,2048]{1,0:T(8,128)(2,1)} %res_ref.1, bf16[4096]{0:T(1024)(128)(2,1)} %gain_ref.1), custom_call_target="tpu_custom_call" | custom-call | tf_op jit(solution)/shard_map/pallas_call | solution.py:153
  34.3 0.0 copy-start
  34.3 1.7 %copy.8 = bf16[48,2048]{1,0:T(8,128)(2,1)} copy(bf16[48,2048]{1,0:T(8,128)(2,1)} %get-tuple-element.4) | data formatting | bytes 393216
  35.9 0.0 copy-done
  35.9 0.7 %copy.9 = bf16[48,2048]{1,0:T(8,128)(2,1)} copy(bf16[48,2048]{1,0:T(8,128)(2,1)S(1)} %copy-done) | data formatting | bytes 393216
Async XLA Ops:
  34.3 1.7 %copy-start = (bf16[48,2048]{1,0:T(8,128)(2,1)S(1)}, bf16[48,2048]{1,0:T(8,128)(2,1)}, u32[]{:S(2)}) copy-start(bf16[48,2048]{1,0:T(8,128)(2,1)} %get-tuple-element.5) | copy-start | bytes 589828
where the time goes:
time: 36.8 us; the launch traced here: 36.6 us
  Pallas kernels  33.6 us (91%)
  local copies, waits for them, and re-layouts  2.34 us (6%)
  between operations  0.65 us (2%)
    pallas_call x1, Pallas kernels, shards(): pl.pallas_call(functools.partial(kernel, ny, ngy, nz), out_shape=[jax.Sha...  33.6 us
    unnamed x4, local copies, waits for them, and re-layouts  2.34 us

commit v1 on v0

v1 whole, which is shorter than its diff:
```python
import functools

import jax
import jax.numpy as jnp
from jax import lax
from jax.experimental import pallas as pl
from jax.experimental.pallas import tpu as pltpu
from jax.sharding import PartitionSpec as P

MESH = pl.DeviceIdType.MESH
F32 = jnp.float32
BF16 = jnp.bfloat16
CORES = 2
W_CUTS = 4


def project(nx, ny, nz, head_ref, w_ref, res_ref, hid_ref, inv_ref,
            heads, w_own, w_other, res_v, send_buf, recv, inb, hold, own, sums,
            head_sem, w_sem, res_sem, w_send, w_recv, hx_send, hy_send, fx_send, fy_send, h_recv,
            p_send, p_recv, c_recv, s_send, s_recv):
    y = lax.axis_index("gx")
    gy = lax.axis_index("gy")
    z = lax.axis_index("gz")
    x, core = lax.div(gy, CORES), lax.rem(gy, CORES)
    out_rows, cols = res_ref.shape
    depth, wc = w_ref.shape
    half = nz // 2
    early = (half + 1) // 2
    s = lax.div(z, half)
    u = z + s * (nz - 1 - 2 * z)
    ahead = 1 - 2 * s
    last = half - 1

    def place(dx, dy, zz):
        return (lax.rem(y + dy, ny), lax.rem(x + dx + nx, nx) * CORES + core, zz)

    def target(kind, k):
        if kind == "F":
            return (1 - s) * (nz - 1) + (2 * s - 1) * k
        return s * half + lax.rem(z - s * half + k, half)

    partner = (y, x * CORES + 1 - core, z)
    border = s * half + (1 - s) * last
    facing = (1 - s) * half + s * last
    pl_sig = functools.partial(pl.semaphore_signal, inc=1, device_id_type=MESH)
    barrier = pltpu.get_barrier_semaphore()
    pl_sig(barrier, device_id=partner)
    pl_sig(barrier, device_id=place(0, 1, z))
    for dx in range(nx):
        for k in range(half):
            if (dx, k) != (0, 0):
                pl_sig(barrier, device_id=place(dx, 0, target("N", k)))
        pl_sig(barrier, device_id=place(dx, 0, facing))

    blocks = [(0, 0)]
    head_in = [pltpu.make_async_copy(head_ref.at[pl.ds(j * out_rows, out_rows)], heads.at[0, y * half + j], head_sem.at[j])
               for j in range(half)]
    step = depth // W_CUTS
    w_in = [pltpu.make_async_copy(w_ref.at[pl.ds(j * step, step)], w_own.at[pl.ds(j * step, step)], w_sem.at[j])
            for j in range(W_CUTS)]
    res_in = pltpu.make_async_copy(res_ref, res_v, res_sem)
    for copy in (*head_in, *w_in, res_in):
        copy.start()
    w_out = [pltpu.make_async_remote_copy(
        src_ref=w_own.at[pl.ds(j * step, step)], dst_ref=w_other.at[pl.ds(j * step, step)],
        send_sem=w_send.at[j], recv_sem=w_recv.at[j], device_id=partner, device_id_type=MESH) for j in range(W_CUTS)]
    for copy in head_in:
        copy.wait()
    met = 2 + nx * half - 1
    pl.semaphore_wait(barrier, met + jnp.where(u == last, nx * half, 0))

    def head_x(dx, t):
        return pltpu.make_async_remote_copy(
            src_ref=heads.at[0, t], dst_ref=heads.at[dx, t], send_sem=hx_send.at[dx, t], recv_sem=h_recv.at[dx, t],
            device_id=place(-dx, 0, z), device_id_type=MESH)

    def head_y(t):
        return pltpu.make_async_remote_copy(
            src_ref=heads.at[0, t], dst_ref=heads.at[0, t], send_sem=hy_send.at[t], recv_sem=h_recv.at[0, t],
            device_id=place(0, 1, z), device_id_type=MESH)

    def onward_y(dx, t):
        return pltpu.make_async_remote_copy(
            src_ref=heads.at[dx, t], dst_ref=heads.at[dx, t], send_sem=fy_send.at[dx, t], recv_sem=h_recv.at[dx, t],
            device_id=place(0, 1, z), device_id_type=MESH)

    def onward_x(dx, t):
        return pltpu.make_async_remote_copy(
            src_ref=heads.at[0, t], dst_ref=heads.at[dx, t], send_sem=fx_send.at[dx, t], recv_sem=h_recv.at[dx, t],
            device_id=place(-dx, 0, z), device_id_type=MESH)

    def landed(dx, t):
        head_x(dx, t).wait_recv()

    def slot(kind, k):
        return k if kind == "F" else half + k

    def to_owner(dx, kind, k, hr):
        n = slot(kind, k)
        return pltpu.make_async_remote_copy(
            src_ref=send_buf.at[dx, n, hr], dst_ref=recv.at[dx, half if kind == "F" else k, hr],
            send_sem=p_send.at[dx, n, hr], recv_sem=p_recv.at[dx, half if kind == "F" else k, hr],
            device_id=place(dx, 0, target(kind, k)), device_id_type=MESH)

    def to_next(dx, k, hr):
        return pltpu.make_async_remote_copy(
            src_ref=send_buf.at[dx, k, hr], dst_ref=inb.at[dx, k, hr],
            send_sem=p_send.at[dx, k, hr], recv_sem=c_recv.at[dx, k, hr],
            device_id=place(0, 0, z + ahead), device_id_type=MESH)

    def compute(dx, kind, k, hr):
        part = jnp.dot(heads[dx, target(kind, k)], (w_other if hr else w_own)[...], preferred_element_type=F32)
        if kind == "N":
            if (dx, k) == (0, 0):
                own[hr] = part
            else:
                send_buf[dx, slot(kind, k), hr] = part.astype(BF16)
                to_owner(dx, kind, k, hr).start()
        else:
            @pl.when(u == 0)
            def _():
                send_buf[dx, k, hr] = part.astype(BF16)
                to_next(dx, k, hr).start()

            @pl.when(u > 0)
            def _():
                hold[dx, k, hr] = part

    def both(dx, kind, k):
        for hr in range(CORES):
            compute(dx, kind, k, hr)

    def merge(dx, k):
        @pl.when(u > 0)
        def _():
            for hr in range(CORES):
                to_next(dx, k, hr).wait_recv()
                send_buf[dx, k, hr] = (hold[dx, k, hr] + inb[dx, k, hr].astype(F32)).astype(BF16)
                if half > 2:
                    pl.when(u < last)(to_next(dx, k, hr).start)
                pl.when(u == last)(to_owner(dx, "F", k, hr).start)

    near = [(k + 1) % half for k in range(half)]
    far = list(range(half))
    others = range(1, nx)

    def run(mine, theirs, merges):
        (mk, mo), (tk, to) = mine, theirs
        for k in mo:
            t = target(mk, k)
            head_y(t).start()
            for dx in others:
                head_x(dx, t).start()
        for j in range(W_CUTS):
            w_in[j].wait()
            w_out[j].start()
        for k in mo:
            compute(0, mk, k, 0)
        for copy in w_out:
            copy.wait_recv()
        for k in mo:
            compute(0, mk, k, 1)
        for o in range(half):
            def x_side(o=o):
                for dx in others:
                    t = target(mk, mo[o])
                    landed(dx, t)
                    if o < early:
                        onward_y(dx, t).start()
                    both(dx, mk, mo[o])

            def y_side(o=o):
                t = target(tk, to[o])
                landed(0, t)
                if o >= early:
                    for dx in others:
                        onward_x(dx, t).start()
                both(0, tk, to[o])

            if mk == "N":
                y_side()
                x_side()
            else:
                x_side()
                y_side()
        if mk == "F":
            for k in mo:
                merge(0, k)
        for o in range(half):
            for dx in others:
                landed(dx, target(tk, to[o]))
                both(dx, tk, to[o])
        for dx in range(1 if mk == "F" else 0, nx):
            for k in far:
                merge(dx, k)
        for o in range(half):
            t = target(mk, mo[o])
            head_y(t).wait_send()
            for dx in others:
                head_x(dx, t).wait_send()
                if o < early:
                    onward_y(dx, t).wait_send()
                else:
                    onward_x(dx, target(tk, to[o])).wait_send()

    pl.when(y == s)(lambda: run(("N", near), ("F", far), 0))
    pl.when(y != s)(lambda: run(("F", far), ("N", near), 0))

    res_in.wait()
    total = jnp.zeros((out_rows, 128), F32)
    for dx in range(nx):
        from_x = lax.rem(x - dx + nx, nx)
        for hr in range(CORES):
            side = core if hr == 0 else 1 - core
            where = pl.ds(pl.multiple_of((from_x * CORES + side) * wc, wc), wc)
            acc = own[hr] if dx == 0 else None
            for k in range(half + 1):
                if (dx, k) == (0, 0):
                    continue
                pltpu.make_async_remote_copy(
                    src_ref=send_buf.at[0, 0, hr], dst_ref=recv.at[dx, k, hr],
                    send_sem=p_send.at[0, 0, hr], recv_sem=p_recv.at[dx, k, hr],
                    device_id=partner, device_id_type=MESH).wait_recv()
                term = recv[dx, k, hr].astype(F32)
                acc = term if acc is None else acc + term
            hidden = (res_v[:, where].astype(F32) + acc).astype(BF16)
            hid_ref[:, where] = hidden
            wide = hidden.astype(F32)
            square = wide * wide
            for k in range(0, wc, 128):
                total = total + square[:, k:k + 128]
    sums[0] = jnp.broadcast_to(jnp.sum(total, axis=1, keepdims=True), (out_rows, 128))
    swap = pltpu.make_async_remote_copy(
        src_ref=sums.at[0], dst_ref=sums.at[1], send_sem=s_send, recv_sem=s_recv,
        device_id=place(0, 1, z), device_id_type=MESH)
    swap.start()

    for copy in w_out:
        copy.wait_send()
    for dx in range(nx):
        for hr in range(CORES):
            for k in range(half):
                if (dx, k) != (0, 0):
                    to_owner(dx, "N", k, hr).wait_send()
                to_next(dx, k, hr).wait_send()
    swap.wait()
    inv_ref[...] = lax.rsqrt((sums[0] + sums[1]) / (cols * ny) + 1e-05)


def finish(hid_ref, inv_ref, gain_ref, out_hid, out_nrm, nrm, sems):
    y = lax.axis_index("gx")
    cols = hid_ref.shape[1]
    first = pltpu.make_async_copy(hid_ref, out_hid, sems.at[0])
    first.start()
    gain = gain_ref[pl.ds(pl.multiple_of(y * cols, cols), cols)].astype(F32).reshape(1, cols)
    nrm[...] = (hid_ref[...].astype(F32) * inv_ref[:, :1] * gain).astype(BF16)
    second = pltpu.make_async_copy(nrm, out_nrm, sems.at[1])
    second.start()
    first.wait()
    second.wait()


def shards(head_out, out_weight, residual, norm_gain):
    ny, ngy, nz = (lax.axis_size(a) for a in ("gx", "gy", "gz"))
    nx = ngy // CORES
    depth, wc = out_weight.shape
    out_rows, cols = residual.shape
    half = nz // 2
    if ny != 2 or nz % 2 or half < 2:
        raise ValueError("unsupported mesh")
    any_spec = pl.BlockSpec(memory_space=pl.ANY)
    vmem = pl.BlockSpec(memory_space=pltpu.VMEM)
    dma = pltpu.SemaphoreType.DMA
    hidden, inverse = pl.pallas_call(
        functools.partial(project, nx, ny, nz),
        out_shape=[pltpu.VMEM((out_rows, cols), BF16), pltpu.VMEM((out_rows, 128), F32)],
        in_specs=[any_spec] * 3,
        out_specs=[vmem, vmem],
        scratch_shapes=[
            pltpu.VMEM((nx, nz, out_rows, depth), BF16),
            pltpu.VMEM((depth, wc), BF16),
            pltpu.VMEM((depth, wc), BF16),
            pltpu.VMEM((out_rows, cols), BF16),
            pltpu.VMEM((nx, nz, CORES, out_rows, wc), BF16),
            pltpu.VMEM((nx, half + 1, CORES, out_rows, wc), BF16),
            pltpu.VMEM((nx, half, CORES, out_rows, wc), BF16),
            pltpu.VMEM((nx, half, CORES, out_rows, wc), F32),
            pltpu.VMEM((CORES, out_rows, wc), F32),
            pltpu.VMEM((ny, out_rows, 128), F32),
            dma((half,)), dma((W_CUTS,)), dma, dma((W_CUTS,)), dma((W_CUTS,)),
            dma((nx, nz)), dma((nz,)), dma((nx, nz)), dma((nx, nz)), dma((nx, nz)),
            dma((nx, nz, CORES)), dma((nx, half + 1, CORES)), dma((nx, half, CORES)),
            dma, dma,
        ],
        compiler_params=pltpu.CompilerParams(collective_id=0, has_side_effects=True),
    )(head_out, out_weight, residual)
    return pl.pallas_call(
        finish,
        out_shape=[jax.ShapeDtypeStruct((out_rows, cols), BF16)] * 2,
        in_specs=[vmem] * 3,
        out_specs=[any_spec] * 2,
        scratch_shapes=[pltpu.VMEM((out_rows, cols), BF16), dma((2,))],
    )(*(pltpu.with_memory_space_constraint(a, pltpu.VMEM) for a in (hidden, inverse)), norm_gain)


def solution(mesh):
    in_specs = (P(("gy", "gx"), "gz"), P("gz", ("gx", "gy")), P(("gy", "gz"), "gx"), P())
    out_specs = (P(("gy", "gz"), "gx"), P(("gy", "gz"), "gx"))
    return jax.shard_map(shards, mesh=mesh, in_specs=in_specs, out_specs=out_specs, check_vma=False)
```

time: 36.8 us -> 32.1 us (0.87)
  Pallas kernels: 33.6 us -> 31.2 us
  local copies, waits for them, and re-layouts: 2.34 us -> 0 us
    pallas_call x1 -> x2, Pallas kernels: 33.6 us -> 31.2 us  [the longest x1 29.7 us: shards(): pl.pallas_call(functools.partial(project, nx, ny, nz), out_shape=[pltpu.V...]
    unnamed x4 -> x0, local copies, waits for them, and re-layouts: 2.34 us -> none
where the time goes in v1:
time: 32.1 us; the launch traced here: 31.8 us
  Pallas kernels  31.2 us (97%)
  between operations  0.64 us (2%)
    pallas_call x1, Pallas kernels, shards(): pl.pallas_call(functools.partial(project, nx, ny, nz), out_shape=[pltpu.V...  29.7 us
    pallas_call x1, Pallas kernels, shards(): pl.pallas_call(finish, out_shape=[jax.ShapeDtypeStruct((out_rows, cols),...  1.51 us

profile of v1, /device:TPU:0, one launch (start us, length us, event | category | flops | bytes accessed | tf_op | source)
XLA Modules:
  0.0 31.8 jit_solution(277031051305591052)
XLA Ops:
  0.6 29.7 %shard_map.59 = (bf16[48,2048]{1,0:T(8,128)(2,1)S(1)}, f32[48,128]{1,0:T(8,128)S(1)}) custom-call(bf16[96,1024]{1,0:T(8,128)(2,1)} %head_ref.1, bf16[1024,512]{1,0:T(8,128)(2,1)} %w_ref.1, bf16[48,2048]{1,0:T(8,128)(2,1)} %res_ref.1), custom_call_target="tpu_custom_call" | custom-call | tf_op jit(solution)/shard_map/pallas_call | solution.py:274
  30.3 1.5 %shard_map.60 = (bf16[48,2048]{1,0:T(8,128)(2,1)}, bf16[48,2048]{1,0:T(8,128)(2,1)}) custom-call(bf16[48,2048]{1,0:T(8,128)(2,1)S(1)} %get-tuple-element.4.hid_ref, f32[48,128]{1,0:T(8,128)S(1)} %get-tuple-element.5.inv_ref, bf16[4096]{0:T(1024)(128)(2,1)} %gain_ref.1), custom_call_target="tpu_custom_call" | custom-call | tf_op jit(solution)/shard_map/pallas_call | solution.py:297

commit v2 on v1

v2 whole, which is shorter than its diff:
```python
import functools

import jax
import jax.numpy as jnp
from jax import lax
from jax.experimental import pallas as pl
from jax.experimental.pallas import tpu as pltpu
from jax.sharding import PartitionSpec as P

MESH = pl.DeviceIdType.MESH
F32 = jnp.float32
BF16 = jnp.bfloat16
CORES = 2
W_CUTS = 4
FINISH_CUTS = 3


def project(nx, ny, nz, head_ref, w_ref, res_ref, gain_ref, hid_ref, inv_ref, gain_out,
            heads, w_own, w_other, res_v, gain_v, send_buf, recv, inb, hold, own, sums,
            in_sem, w_sem, w_send, w_recv, h_send, h_recv, p_send, n_recv, m_recv, c_recv, s_send, s_recv, up_sem, down_sem):
    y = lax.axis_index("gx")
    gy = lax.axis_index("gy")
    z = lax.axis_index("gz")
    x, core = lax.div(gy, CORES), lax.rem(gy, CORES)
    out_rows, cols = res_ref.shape
    depth, wc = w_ref.shape
    half = nz // 2
    early = (half + 1) // 2
    s = lax.div(z, half)
    u = z + s * (nz - 1 - 2 * z)
    ahead = 1 - 2 * s
    last = half - 1

    def place(dx, dy, zz):
        return (lax.rem(y + dy, ny), lax.rem(x + dx + nx, nx) * CORES + core, zz)

    def target(kind, k):
        if kind == "F":
            return (1 - s) * (nz - 1) + (2 * s - 1) * k
        return s * half + lax.rem(z - s * half + k, half)

    partner = (y, x * CORES + 1 - core, z)
    pl_sig = functools.partial(pl.semaphore_signal, inc=1, device_id_type=MESH)
    barrier = pltpu.get_barrier_semaphore()
    pl_sig(barrier, device_id=partner)
    pl_sig(barrier, device_id=place(0, 1, z))
    for dx in range(1, nx):
        pl_sig(barrier, device_id=place(dx, 0, z))
    below, above = z > 0, z < nz - 1
    pl.when(below)(lambda: pl_sig(barrier, device_id=place(0, 0, z - 1)))
    pl.when(above)(lambda: pl_sig(barrier, device_id=place(0, 0, z + 1)))

    mine = heads.at[pl.ds(y * half, half)]
    head_in = pltpu.make_async_copy(head_ref, mine, in_sem.at[0])
    step = depth // W_CUTS
    w_in = [pltpu.make_async_copy(w_ref.at[pl.ds(j * step, step)], w_own.at[pl.ds(j * step, step)], w_sem.at[j])
            for j in range(W_CUTS)]
    res_in = pltpu.make_async_copy(res_ref, res_v, in_sem.at[1])
    gain_in = pltpu.make_async_copy(gain_ref.at[pl.ds(pl.multiple_of(y * cols, cols), cols)], gain_v, in_sem.at[2])
    for copy in (head_in, *w_in, res_in, gain_in):
        copy.start()
    w_out = [pltpu.make_async_remote_copy(
        src_ref=w_own.at[pl.ds(j * step, step)], dst_ref=w_other.at[pl.ds(j * step, step)],
        send_sem=w_send, recv_sem=w_recv, device_id=partner, device_id_type=MESH) for j in range(W_CUTS)]
    head_in.wait()
    pl.semaphore_wait(barrier, nx + 1 + jnp.minimum(z, 1) + jnp.minimum(nz - 1 - z, 1))

    def pass_up():
        pl.when(below)(lambda: pl.semaphore_wait(up_sem, 1))
        pl.when(above)(lambda: pl_sig(up_sem, device_id=place(0, 0, z + 1)))

    def pass_down():
        pl.when(above)(lambda: pl.semaphore_wait(down_sem, 1))
        pl.when(below)(lambda: pl_sig(down_sem, device_id=place(0, 0, z - 1)))

    def meet_first():
        pl.when(s == 0)(pass_up)
        pl.when(s == 1)(pass_down)

    def meet_last():
        pl.when(s == 0)(pass_down)
        pl.when(s == 1)(pass_up)

    all_w = pltpu.make_async_remote_copy(
        src_ref=w_own, dst_ref=w_other, send_sem=w_send, recv_sem=w_recv, device_id=partner, device_id_type=MESH)

    def hop(source, dest, t, to):
        return pltpu.make_async_remote_copy(
            src_ref=heads.at[source * nz + t], dst_ref=heads.at[dest * nz + t], send_sem=h_send,
            recv_sem=h_recv.at[dest, t], device_id=to, device_id_type=MESH)

    def head_x(dx, t):
        return hop(0, dx, t, place(-dx, 0, z))

    def head_y(t):
        return hop(0, 0, t, place(0, 1, z))

    def onward_y(dx, t):
        return hop(dx, dx, t, place(0, 1, z))

    onward_x = head_x

    def landed(dx, t):
        head_x(dx, t).wait_recv()

    def slot(dx, kind, k):
        return dx * nz + (half + k if kind == "F" else k) - 1

    def arrival(dx, kind, k, hr):
        return m_recv.at[dx, hr] if kind == "F" else n_recv.at[dx]

    def to_owner(dx, kind, k, hr):
        return pltpu.make_async_remote_copy(
            src_ref=send_buf.at[slot(dx, kind, k), hr], dst_ref=recv.at[dx, half if kind == "F" else k, hr],
            send_sem=p_send, recv_sem=arrival(dx, kind, k, hr), device_id=place(dx, 0, target(kind, k)), device_id_type=MESH)

    def to_next(dx, k, hr):
        return pltpu.make_async_remote_copy(
            src_ref=send_buf.at[slot(dx, "F", k), hr], dst_ref=inb.at[dx, k, hr],
            send_sem=p_send, recv_sem=c_recv.at[dx, k, hr], device_id=place(0, 0, z + ahead), device_id_type=MESH)

    def compute(dx, kind, k, hr, send=True):
        part = jnp.dot(heads[dx * nz + target(kind, k)], (w_other if hr else w_own)[...], preferred_element_type=F32)
        if kind == "N":
            if (dx, k) == (0, 0):
                own[hr] = part
            else:
                send_buf[slot(dx, kind, k), hr] = part.astype(BF16)
                if send:
                    to_owner(dx, kind, k, hr).start()
                else:
                    pl.when(u > 0)(to_owner(dx, kind, k, hr).start)
        else:
            @pl.when(u == 0)
            def _():
                send_buf[slot(dx, "F", k), hr] = part.astype(BF16)
                to_next(dx, k, hr).start()

            @pl.when(u > 0)
            def _():
                hold[dx, k, hr] = part

    def both(dx, kind, k, send=True):
        for hr in range(CORES):
            compute(dx, kind, k, hr, send)

    def late(dx, k):
        for hr in range(CORES):
            pl.when(u == 0)(to_owner(dx, "N", k, hr).start)

    def merge(dx, k):
        @pl.when(u > 0)
        def _():
            for hr in range(CORES):
                to_next(dx, k, hr).wait_recv()
                send_buf[slot(dx, "F", k), hr] = (hold[dx, k, hr] + inb[dx, k, hr].astype(F32)).astype(BF16)
                if half > 2:
                    pl.when(u < last)(to_next(dx, k, hr).start)
                pl.when(u == last)(to_owner(dx, "F", k, hr).start)

    near = far = list(range(half))
    others = range(1, nx)

    def run(local, distant):
        (mk, mo), (tk, to) = local, distant

        def x_out(o):
            for dx in others:
                head_x(dx, target(mk, mo[o])).start()

        for o in range(half):
            head_y(target(mk, mo[o])).start()
            r = half - 1 - o
            if mk == "F" or r >= early:
                x_out(r)
        for j in range(W_CUTS):
            w_in[j].wait()
            w_out[j].start()
        meet_first()
        if half > 2:
            meet_last()
        for k in reversed(mo) if mk == "N" else mo:
            compute(0, mk, k, 0)
        all_w.wait_recv()
        for k in reversed(mo) if mk == "N" else mo:
            compute(0, mk, k, 1)

        def x_land(o):
            for dx in others:
                t = target(mk, mo[o])
                landed(dx, t)
                if o >= early:
                    onward_y(dx, t).start()

        def y_land(o):
            t = target(tk, to[o])
            landed(0, t)
            if o < early:
                for dx in others:
                    onward_x(dx, t).start()

        def diagonal(o):
            for dx in others:
                landed(dx, target(tk, to[o]))
                both(dx, tk, to[o])

        if mk == "N":
            for o in range(half):
                y_land(o)
                if o < early:
                    x_out(early - 1 - o)
                both(0, tk, to[o])
                if half - 1 - o >= early:
                    x_land(half - 1 - o)
        else:
            for o in range(half):
                x_land(half - 1 - o)
                for dx in others:
                    both(dx, mk, mo[half - 1 - o])
                y_land(o)
        if half == 2:
            meet_last()
        if mk == "N":
            for r in reversed(range(early, half)):
                for dx in others:
                    both(dx, mk, mo[r], send=False)
            merge(0, far[0])
            for o in range(half):
                diagonal(o)
            for k in far[1:]:
                merge(0, k)
            for r in reversed(range(early)):
                x_land(r)
                for dx in others:
                    both(dx, mk, mo[r], send=mo[r] == 0)
            for k in far:
                for dx in others:
                    merge(dx, k)
            for k in range(1, half):
                for dx in others:
                    late(dx, k)
        else:
            for k in far:
                merge(0, k)
                both(0, tk, to[half - 1 - k])
            for o in reversed(range(half)):
                diagonal(o)
            for k in reversed(far):
                for dx in others:
                    merge(dx, k)

    pl.when(y == s)(lambda: run(("N", near), ("F", far)))
    pl.when(y != s)(lambda: run(("F", far), ("N", near)))

    gain_in.wait()
    gain_out[...] = gain_v[...].astype(F32).reshape(1, cols)
    res_in.wait()
    total = jnp.zeros((out_rows, 128), F32)
    for dx in range(nx):
        from_x = lax.rem(x - dx + nx, nx)
        for hr in range(CORES):
            side = core if hr == 0 else 1 - core
            where = pl.ds(pl.multiple_of((from_x * CORES + side) * wc, wc), wc)
            if hr == 0:
                group = recv.at[dx, pl.ds(1 if dx == 0 else 0, half - 1 if dx == 0 else half)]
                pltpu.make_async_remote_copy(
                    src_ref=group, dst_ref=group, send_sem=p_send, recv_sem=n_recv.at[dx],
                    device_id=partner, device_id_type=MESH).wait_recv()
            acc = own[hr] if dx == 0 else recv[dx, 0, hr].astype(F32)
            for k in range(1, half):
                acc = acc + recv[dx, k, hr].astype(F32)
            to_owner(dx, "F", 0, hr).wait_recv()
            acc = acc + recv[dx, half, hr].astype(F32)
            hidden = (res_v[:, where].astype(F32) + acc).astype(BF16)
            hid_ref[:, where] = hidden
            wide = hidden.astype(F32)
            square = wide * wide
            for k in range(0, wc, 128):
                total = total + square[:, k:k + 128]
    sums[0] = jnp.broadcast_to(jnp.sum(total, axis=1, keepdims=True), (out_rows, 128))
    swap = pltpu.make_async_remote_copy(
        src_ref=sums.at[0], dst_ref=sums.at[1], send_sem=s_send, recv_sem=s_recv,
        device_id=place(0, 1, z), device_id_type=MESH)
    swap.start()

    all_w.wait_send()
    sent = heads.at[pl.ds(0, nx * nz - half)]
    for buf, sem in ((sent, h_send), (send_buf, p_send)):
        pltpu.make_async_remote_copy(
            src_ref=buf, dst_ref=buf, send_sem=sem, recv_sem=w_recv, device_id=partner, device_id_type=MESH).wait_send()
    swap.wait()
    inv_ref[...] = lax.rsqrt((sums[0] + sums[1]) / (cols * ny) + 1e-05)


def finish(hid_ref, inv_ref, gain_ref, out_hid, out_nrm, nrm, sems):
    rows, cols = hid_ref.shape
    cut = rows // FINISH_CUTS
    whole = pltpu.make_async_copy(hid_ref, out_hid, sems.at[FINISH_CUTS])
    whole.start()
    parts = []
    for j in range(FINISH_CUTS):
        at = pl.ds(j * cut, cut)
        nrm[at] = (hid_ref[at].astype(F32) * inv_ref[at, :1] * gain_ref[...]).astype(BF16)
        parts.append(pltpu.make_async_copy(nrm.at[at], out_nrm.at[at], sems.at[j]))
        parts[-1].start()
    for copy in (whole, *parts):
        copy.wait()


def shards(head_out, out_weight, residual, norm_gain):
    ny, ngy, nz = (lax.axis_size(a) for a in ("gx", "gy", "gz"))
    nx = ngy // CORES
    depth, wc = out_weight.shape
    out_rows, cols = residual.shape
    half = nz // 2
    if ny != 2 or nz % 2 or half < 2:
        raise ValueError("unsupported mesh")
    any_spec = pl.BlockSpec(memory_space=pl.ANY)
    vmem = pl.BlockSpec(memory_space=pltpu.VMEM)
    dma, regular = pltpu.SemaphoreType.DMA, pltpu.SemaphoreType.REGULAR
    held = pl.pallas_call(
        functools.partial(project, nx, ny, nz),
        out_shape=[pltpu.VMEM((out_rows, cols), BF16), pltpu.VMEM((out_rows, 128), F32), pltpu.VMEM((1, cols), F32)],
        in_specs=[any_spec] * 4,
        out_specs=[vmem] * 3,
        scratch_shapes=[
            pltpu.VMEM((nx * nz, out_rows, depth), BF16),
            pltpu.VMEM((depth, wc), BF16),
            pltpu.VMEM((depth, wc), BF16),
            pltpu.VMEM((out_rows, cols), BF16),
            pltpu.VMEM((cols,), BF16),
            pltpu.VMEM((nx * nz - 1, CORES, out_rows, wc), BF16),
            pltpu.VMEM((nx, half + 1, CORES, out_rows, wc), BF16),
            pltpu.VMEM((nx, half, CORES, out_rows, wc), BF16),
            pltpu.VMEM((nx, half, CORES, out_rows, wc), F32),
            pltpu.VMEM((CORES, out_rows, wc), F32),
            pltpu.VMEM((ny, out_rows, 128), F32),
            dma((3,)), dma((W_CUTS,)), dma, dma, dma, dma((nx, nz)),
            dma, dma((nx,)), dma((nx, CORES)), dma((nx, half, CORES)), dma, dma, regular, regular,
        ],
        compiler_params=pltpu.CompilerParams(collective_id=0, has_side_effects=True),
    )(head_out.reshape(half, out_rows, depth), out_weight, residual, norm_gain)
    return pl.pallas_call(
        finish,
        out_shape=[jax.ShapeDtypeStruct((out_rows, cols), BF16)] * 2,
        in_specs=[vmem] * 3,
        out_specs=[any_spec] * 2,
        scratch_shapes=[pltpu.VMEM((out_rows, cols), BF16), dma((FINISH_CUTS + 1,))],
    )(*(pltpu.with_memory_space_constraint(a, pltpu.VMEM) for a in held))


def solution(mesh):
    in_specs = (P(("gy", "gx"), "gz"), P("gz", ("gx", "gy")), P(("gy", "gz"), "gx"), P())
    out_specs = (P(("gy", "gz"), "gx"), P(("gy", "gz"), "gx"))
    return jax.shard_map(shards, mesh=mesh, in_specs=in_specs, out_specs=out_specs, check_vma=False)
```

time: 32.1 us -> 28.4 us (0.88)
  Pallas kernels: 31.2 us -> 27.6 us
    pallas_call x1, Pallas kernels: 29.7 us -> 26.8 us  [shards(): pl.pallas_call(functools.partial(project, nx, ny, nz), out_shape=[pltpu.V...]
    pallas_call x1, Pallas kernels: 1.51 us -> 0.81 us  [shards(): pl.pallas_call(finish, out_shape=[jax.ShapeDtypeStruct((out_rows, cols),...]
where the time goes in v2:
time: 28.4 us; the launch traced here: 28.2 us
  Pallas kernels  27.6 us (97%)
  between operations  0.64 us (2%)
    pallas_call x1, Pallas kernels, shards(): pl.pallas_call(functools.partial(project, nx, ny, nz), out_shape=[pltpu.V...  26.8 us
    pallas_call x1, Pallas kernels, shards(): pl.pallas_call(finish, out_shape=[jax.ShapeDtypeStruct((out_rows, cols),...  0.81 us

profile of v2, /device:TPU:0, one launch (start us, length us, event | category | flops | bytes accessed | tf_op | source)
XLA Modules:
  0.0 28.2 jit_solution(12051731268701109021)
XLA Ops:
  0.6 26.8 %shard_map.59 = (bf16[48,2048]{1,0:T(8,128)(2,1)S(1)}, f32[48,128]{1,0:T(8,128)S(1)}, f32[1,2048]{1,0:T(1,128)S(1)}) custom-call(bf16[2,48,1024]{2,1,0:T(8,128)(2,1)} %bitcast.1, bf16[1024,512]{1,0:T(8,128)(2,1)} %w_ref.1, bf16[48,2048]{1,0:T(8,128)(2,1)} %res_ref.1, bf16[4096]{0:T(1024)(128)(2,1)} %gain_ref.1), custom_call_target="tpu_custom_call" | custom-call | tf_op jit(solution)/shard_map/pallas_call | solution.py:321
  27.4 0.8 %shard_map.60 = (bf16[48,2048]{1,0:T(8,128)(2,1)}, bf16[48,2048]{1,0:T(8,128)(2,1)}) custom-call(bf16[48,2048]{1,0:T(8,128)(2,1)S(1)} %get-tuple-element.5.hid_ref, f32[48,128]{1,0:T(8,128)S(1)} %get-tuple-element.6.inv_ref, f32[1,2048]{1,0:T(1,128)S(1)} %get-tuple-element.7.gain_ref), custom_call_target="tpu_custom_call" | custom-call | tf_op jit(solution)/shard_map/pallas_call | solution.py:343

commit v3 on v2

--- a/solution.py
+++ b/solution.py
@@ -16,7 +16,7 @@
 
 
 def project(nx, ny, nz, head_ref, w_ref, res_ref, gain_ref, hid_ref, inv_ref, gain_out,
-            heads, w_own, w_other, res_v, gain_v, send_buf, recv, inb, hold, own, sums,
+            mine, heads, w_own, w_other, res_v, gain_v, send_buf, recv, inb, hold, sums,
             in_sem, w_sem, w_send, w_recv, h_send, h_recv, p_send, n_recv, m_recv, c_recv, s_send, s_recv, up_sem, down_sem):
     y = lax.axis_index("gx")
     gy = lax.axis_index("gy")
@@ -31,26 +31,27 @@
     ahead = 1 - 2 * s
     last = half - 1
 
-    def place(dx, dy, zz):
-        return (lax.rem(y + dy, ny), lax.rem(x + dx + nx, nx) * CORES + core, zz)
+    def place(dx, dy, zz, side=core):
+        return (lax.rem(y + dy, ny), lax.rem(x + dx + nx, nx) * CORES + side, zz)
 
     def target(kind, k):
         if kind == "F":
             return (1 - s) * (nz - 1) + (2 * s - 1) * k
         return s * half + lax.rem(z - s * half + k, half)
 
-    partner = (y, x * CORES + 1 - core, z)
+    cross = 1 - core
+    partner = place(0, 0, z, cross)
     pl_sig = functools.partial(pl.semaphore_signal, inc=1, device_id_type=MESH)
     barrier = pltpu.get_barrier_semaphore()
     pl_sig(barrier, device_id=partner)
-    pl_sig(barrier, device_id=place(0, 1, z))
-    for dx in range(1, nx):
-        pl_sig(barrier, device_id=place(dx, 0, z))
     below, above = z > 0, z < nz - 1
-    pl.when(below)(lambda: pl_sig(barrier, device_id=place(0, 0, z - 1)))
-    pl.when(above)(lambda: pl_sig(barrier, device_id=place(0, 0, z + 1)))
-
-    mine = heads.at[pl.ds(y * half, half)]
+    for side in (core, cross):
+        pl_sig(barrier, device_id=place(0, 1, z, side))
+        for dx in range(1, nx):
+            pl_sig(barrier, device_id=place(dx, 0, z, side))
+        pl.when(below)(lambda: pl_sig(barrier, device_id=place(0, 0, z - 1, side)))
+        pl.when(above)(lambda: pl_sig(barrier, device_id=place(0, 0, z + 1, side)))
+
     head_in = pltpu.make_async_copy(head_ref, mine, in_sem.at[0])
     step = depth // W_CUTS
     w_in = [pltpu.make_async_copy(w_ref.at[pl.ds(j * step, step)], w_own.at[pl.ds(j * step, step)], w_sem.at[j])
@@ -63,7 +64,7 @@
         src_ref=w_own.at[pl.ds(j * step, step)], dst_ref=w_other.at[pl.ds(j * step, step)],
         send_sem=w_send, recv_sem=w_recv, device_id=partner, device_id_type=MESH) for j in range(W_CUTS)]
     head_in.wait()
-    pl.semaphore_wait(barrier, nx + 1 + jnp.minimum(z, 1) + jnp.minimum(nz - 1 - z, 1))
+    pl.semaphore_wait(barrier, 1 + CORES * (nx + jnp.minimum(z, 1) + jnp.minimum(nz - 1 - z, 1)))
 
     def pass_up():
         pl.when(below)(lambda: pl.semaphore_wait(up_sem, 1))
@@ -84,27 +85,25 @@
     all_w = pltpu.make_async_remote_copy(
         src_ref=w_own, dst_ref=w_other, send_sem=w_send, recv_sem=w_recv, device_id=partner, device_id_type=MESH)
 
-    def hop(source, dest, t, to):
+    def hop(source, dx, t, to):
         return pltpu.make_async_remote_copy(
-            src_ref=heads.at[source * nz + t], dst_ref=heads.at[dest * nz + t], send_sem=h_send,
-            recv_sem=h_recv.at[dest, t], device_id=to, device_id_type=MESH)
-
-    def head_x(dx, t):
-        return hop(0, dx, t, place(-dx, 0, z))
-
-    def head_y(t):
-        return hop(0, 0, t, place(0, 1, z))
+            src_ref=source, dst_ref=heads.at[dx * nz + t], send_sem=h_send,
+            recv_sem=h_recv.at[dx, t], device_id=to, device_id_type=MESH)
+
+    def head_out(dx, dy, t):
+        return hop(mine.at[t - y * half], dx, t, place(-dx, dy, z, cross))
 
     def onward_y(dx, t):
-        return hop(dx, dx, t, place(0, 1, z))
-
-    onward_x = head_x
+        return hop(heads.at[dx * nz + t], dx, t, place(0, 1, z))
+
+    def onward_x(dx, t):
+        return hop(heads.at[t], dx, t, place(-dx, 0, z))
 
     def landed(dx, t):
-        head_x(dx, t).wait_recv()
+        onward_y(dx, t).wait_recv()
 
     def slot(dx, kind, k):
-        return dx * nz + (half + k if kind == "F" else k) - 1
+        return dx * nz + (half + k if kind == "F" else k)
 
     def arrival(dx, kind, k, hr):
         return m_recv.at[dx, hr] if kind == "F" else n_recv.at[dx]
@@ -112,7 +111,7 @@
     def to_owner(dx, kind, k, hr):
         return pltpu.make_async_remote_copy(
             src_ref=send_buf.at[slot(dx, kind, k), hr], dst_ref=recv.at[dx, half if kind == "F" else k, hr],
-            send_sem=p_send, recv_sem=arrival(dx, kind, k, hr), device_id=place(dx, 0, target(kind, k)), device_id_type=MESH)
+            send_sem=p_send, recv_sem=arrival(dx, kind, k, hr), device_id=place(dx, 0, target(kind, k), cross), device_id_type=MESH)
 
     def to_next(dx, k, hr):
         return pltpu.make_async_remote_copy(
@@ -122,14 +121,11 @@
     def compute(dx, kind, k, hr, send=True):
         part = jnp.dot(heads[dx * nz + target(kind, k)], (w_other if hr else w_own)[...], preferred_element_type=F32)
         if kind == "N":
-            if (dx, k) == (0, 0):
-                own[hr] = part
+            send_buf[slot(dx, kind, k), hr] = part.astype(BF16)
+            if send:
+                to_owner(dx, kind, k, hr).start()
             else:
-                send_buf[slot(dx, kind, k), hr] = part.astype(BF16)
-                if send:
-                    to_owner(dx, kind, k, hr).start()
-                else:
-                    pl.when(u > 0)(to_owner(dx, kind, k, hr).start)
+                pl.when(u > 0)(to_owner(dx, kind, k, hr).start)
         else:
             @pl.when(u == 0)
             def _():
@@ -166,10 +162,12 @@
 
         def x_out(o):
             for dx in others:
-                head_x(dx, target(mk, mo[o])).start()
-
+                head_out(dx, 0, target(mk, mo[o])).start()
+
+        for o in reversed(range(half)) if mk == "N" else range(half):
+            head_out(0, 0, target(mk, mo[o])).start()
         for o in range(half):
-            head_y(target(mk, mo[o])).start()
+            head_out(0, 1, target(mk, mo[o])).start()
             r = half - 1 - o
             if mk == "F" or r >= early:
                 x_out(r)
@@ -180,6 +178,7 @@
         if half > 2:
             meet_last()
         for k in reversed(mo) if mk == "N" else mo:
+            landed(0, target(mk, k))
             compute(0, mk, k, 0)
         all_w.wait_recv()
         for k in reversed(mo) if mk == "N" else mo:
@@ -259,14 +258,14 @@
     for dx in range(nx):
         from_x = lax.rem(x - dx + nx, nx)
         for hr in range(CORES):
-            side = core if hr == 0 else 1 - core
+            side = cross if hr == 0 else core
             where = pl.ds(pl.multiple_of((from_x * CORES + side) * wc, wc), wc)
             if hr == 0:
-                group = recv.at[dx, pl.ds(1 if dx == 0 else 0, half - 1 if dx == 0 else half)]
+                group = recv.at[dx, pl.ds(0, half)]
                 pltpu.make_async_remote_copy(
                     src_ref=group, dst_ref=group, send_sem=p_send, recv_sem=n_recv.at[dx],
                     device_id=partner, device_id_type=MESH).wait_recv()
-            acc = own[hr] if dx == 0 else recv[dx, 0, hr].astype(F32)
+            acc = recv[dx, 0, hr].astype(F32)
             for k in range(1, half):
                 acc = acc + recv[dx, k, hr].astype(F32)
             to_owner(dx, "F", 0, hr).wait_recv()
@@ -284,8 +283,7 @@
     swap.start()
 
     all_w.wait_send()
-    sent = heads.at[pl.ds(0, nx * nz - half)]
-    for buf, sem in ((sent, h_send), (send_buf, p_send)):
+    for buf, sem in ((heads, h_send), (send_buf, p_send)):
         pltpu.make_async_remote_copy(
             src_ref=buf, dst_ref=buf, send_sem=sem, recv_sem=w_recv, device_id=partner, device_id_type=MESH).wait_send()
     swap.wait()
@@ -324,16 +322,16 @@
         in_specs=[any_spec] * 4,
         out_specs=[vmem] * 3,
         scratch_shapes=[
+            pltpu.VMEM((half, out_rows, depth), BF16),
             pltpu.VMEM((nx * nz, out_rows, depth), BF16),
             pltpu.VMEM((depth, wc), BF16),
             pltpu.VMEM((depth, wc), BF16),
             pltpu.VMEM((out_rows, cols), BF16),
             pltpu.VMEM((cols,), BF16),
-            pltpu.VMEM((nx * nz - 1, CORES, out_rows, wc), BF16),
+            pltpu.VMEM((nx * nz, CORES, out_rows, wc), BF16),
             pltpu.VMEM((nx, half + 1, CORES, out_rows, wc), BF16),
             pltpu.VMEM((nx, half, CORES, out_rows, wc), BF16),
             pltpu.VMEM((nx, half, CORES, out_rows, wc), F32),
-            pltpu.VMEM((CORES, out_rows, wc), F32),
             pltpu.VMEM((ny, out_rows, 128), F32),
             dma((3,)), dma((W_CUTS,)), dma, dma, dma, dma((nx, nz)),
             dma, dma((nx,)), dma((nx, CORES)), dma((nx, half, CORES)), dma, dma, regular, regular,

time: 28.4 us -> 26.7 us (0.940)
  Pallas kernels: 27.6 us -> 25.9 us
    pallas_call x1, Pallas kernels: 26.8 us -> 25.1 us  [shards(): pl.pallas_call(functools.partial(project, nx, ny, nz), out_shape=[pltpu.V...]
where the time goes in v3:
time: 26.7 us; the launch traced here: 26.5 us
  Pallas kernels  25.9 us (97%)
  between operations  0.64 us (2%)
    pallas_call x1, Pallas kernels, shards(): pl.pallas_call(functools.partial(project, nx, ny, nz), out_shape=[pltpu.V...  25.1 us
    pallas_call x1, Pallas kernels, shards(): pl.pallas_call(finish, out_shape=[jax.ShapeDtypeStruct((out_rows, cols),...  0.81 us

profile of v3, /device:TPU:0, one launch (start us, length us, event | category | flops | bytes accessed | tf_op | source)
XLA Modules:
  0.0 26.5 jit_solution(10039058640990700246)
XLA Ops:
  0.6 25.1 %shard_map.59 = (bf16[48,2048]{1,0:T(8,128)(2,1)S(1)}, f32[48,128]{1,0:T(8,128)S(1)}, f32[1,2048]{1,0:T(1,128)S(1)}) custom-call(bf16[2,48,1024]{2,1,0:T(8,128)(2,1)} %bitcast.1, bf16[1024,512]{1,0:T(8,128)(2,1)} %w_ref.1, bf16[48,2048]{1,0:T(8,128)(2,1)} %res_ref.1, bf16[4096]{0:T(1024)(128)(2,1)} %gain_ref.1), custom_call_target="tpu_custom_call" | custom-call | tf_op jit(solution)/shard_map/pallas_call | solution.py:319
  25.7 0.8 %shard_map.60 = (bf16[48,2048]{1,0:T(8,128)(2,1)}, bf16[48,2048]{1,0:T(8,128)(2,1)}) custom-call(bf16[48,2048]{1,0:T(8,128)(2,1)S(1)} %get-tuple-element.5.hid_ref, f32[48,128]{1,0:T(8,128)S(1)} %get-tuple-element.6.inv_ref, f32[1,2048]{1,0:T(1,128)S(1)} %get-tuple-element.7.gain_ref), custom_call_target="tpu_custom_call" | custom-call | tf_op jit(solution)/shard_map/pallas_call | solution.py:341
